TPU v7x, 512 devices: a whole 4x4x16 slice. The times are simulated.
512 devices in a mesh: seq: 32 (over z, core), mp: 4 (over x), batch: 4 (over y).
Axes of the slice: x: 4, y: 4, z: 16, core: 2. Of those that a mesh axis runs over, the one named last changes fastest.
Arguments:
- queries: bfloat16 [4, 128, 4096], P('batch', 'seq', 'mp'), may hold values from -6 to 6
- keys: bfloat16 [4, 8192, 1024], P('batch', 'seq', 'mp'), may hold values from -6 to 6
- values: bfloat16 [4, 8192, 1024], P('batch', 'seq', 'mp'), may hold values from -6 to 6
- key_position: float32 [32, 128], replicated, may hold values from -4 to 4
- compress_keys: bfloat16 [4096, 128], replicated, may hold values from -0.2 to 0.2
- compress_values: bfloat16 [4096, 128], replicated, may hold values from -0.09375 to 0.09375
- out_proj: bfloat16 [4096, 4096], P('mp', 'seq'), may hold values from -0.09375 to 0.09375
- residual: bfloat16 [4, 128, 4096], P(None, None, 'seq'), may hold values from -6 to 6
- norm_gain: float32 [4096], replicated, may hold values from 0.25 to 1.75
- lm_head: bfloat16 [131072, 4096], P(('seq', 'mp', 'batch')), may hold values from -0.4 to 0.4
- targets: int32 [4, 128], replicated, may hold values from 0 to 131071
- lengths: int32 [4], replicated, may hold values from 2048 to 8192
Outputs:
- token_logprob: float32 [4, 128], P('batch', 'seq')
- rollout_score: float32 [4], P('batch')
All inputs are finite; a program needn't handle non-finite values.
Results may differ from a plain program's by a relative error of at most 0.0005.
The roundings to bfloat16 on the way count: a program that leaves them out, or rounds other values in their place, can miss the bound.
Values may be sent and summed in bfloat16 or wider, within the bound.
A program may use at most 64 MiB of HBM per device.

v0:
```python
import math

import jax
import jax.numpy as jnp
from jax import lax
from jax.sharding import Mesh
from jax.sharding import PartitionSpec as P

HEAD_DIM = 128
BLOCK = 32
STRIDE = 16
SEQ = ("seq_0", "seq_1")
SEQ_MP = ("seq_0", "seq_1", "mp")
SEQ_MP_BATCH = ("seq_0", "seq_1", "mp", "batch")


def from_behind(block, axis, distance):
    devices = range(lax.axis_size(axis))
    route = [(i - distance, i) for i in devices if i - distance in devices]
    return lax.ppermute(block, axis, route)


def joined_along(tiles, dim):
    lengths = list(tiles.shape[1:])
    lengths[dim] *= tiles.shape[0]
    return jnp.moveaxis(tiles, 0, dim).reshape(lengths)


def copy_for_each(array, axis):
    copies = jnp.broadcast_to(array, (lax.axis_size(axis), *array.shape))
    return lax.all_to_all(copies, axis, split_axis=0, concat_axis=0, tiled=True)


def collect(array, axis, dim):
    return joined_along(copy_for_each(array, axis), dim)


def taken_together(array, axis):
    return copy_for_each(array, axis).sum(axis=0)


def all_in_one(array, axis):
    leaves = jax.tree.leaves(array)
    turns = sorted(range(len(leaves)), key=lambda k: -leaves[k].size)
    width = (1, *leaves[turns[0]].shape)[-1]
    lines = [
        jnp.pad(leaves[k].reshape(-1), (0, -leaves[k].size % width)).reshape(-1, width)
        for k in turns
    ]
    both, at, found = (lax.all_gather(jnp.concatenate(lines), axis), 0, {})
    for k, line in zip(turns, lines):
        slab = both[:, at : at + len(line)].reshape(len(both), -1)
        found[k] = slab[:, : leaves[k].size].reshape(-1, *leaves[k].shape)
        at += len(line)
    numbers = iter(range(len(leaves)))
    return jax.tree.map(lambda _: found[next(numbers)], array)


def combined_by_axis(array, axes, combine):
    for axis in axes:
        pieces = all_in_one(array, axis)
        array = jax.tree.map(lambda part: part[0], pieces)
        for k in range(1, lax.axis_size(axis)):
            array = combine(array, jax.tree.map(lambda part: part[k], pieces))
    return array


def compress_rows(rows, following, position, weight):
    extended = jnp.concatenate([rows, following], 0)
    count = rows.shape[0] // STRIDE
    heads = rows.shape[1] // HEAD_DIM
    shaped = extended.reshape(count + 1, STRIDE, heads, HEAD_DIM)
    blocks = jnp.concatenate([shaped[:-1], shaped[1:]], 1)
    blocks = (blocks.astype(jnp.float32) + position[None, :, None, :]).astype(jnp.bfloat16)
    mapped = jnp.einsum(
        "bjhd,jde->bhe",
        blocks,
        weight.reshape(BLOCK, HEAD_DIM, HEAD_DIM),
        preferred_element_type=jnp.float32,
    )
    return mapped.astype(jnp.bfloat16).reshape(count, heads * HEAD_DIM)


def normalize(hidden, gain):
    widened = hidden.astype(jnp.float32)
    meansq = jnp.mean(widened * widened, -1, keepdims=True)
    return (widened * lax.rsqrt(meansq + 1e-05) * gain).astype(jnp.bfloat16)


def vocab_logits(normed, rows):
    return lax.dot_general(
        normed, rows, (((1,), (1,)), ((), ())), preferred_element_type=jnp.float32
    )


def picked_logit(logits, offset, wanted):
    columns = offset + jnp.arange(logits.shape[1], dtype=jnp.int32)
    hits = columns[None, :] == wanted[:, None]
    return jnp.sum(jnp.where(hits, logits, 0.0), 1)


def join_terms(first, second):
    top = jnp.maximum(first[0], second[0])
    total = first[1] * jnp.exp(first[0] - top) + second[1] * jnp.exp(second[0] - top)
    return (top, total, first[2] + second[2])


def body(
    queries,
    keys,
    values,
    key_position,
    compress_keys,
    compress_values,
    out_proj,
    residual,
    norm_gain,
    lm_head,
    targets,
    lengths,
):
    seq_pos = lax.axis_index(SEQ)
    batch_count = lax.axis_size("batch")
    batch_pos = lax.axis_index("batch")
    qcount = queries.shape[1]
    skip = keys.shape[1] // qcount
    scored = targets.shape[1]
    following = from_behind((keys[0, :STRIDE], values[0, :STRIDE]), SEQ, -1)
    comp_keys = compress_rows(keys[0], following[0], key_position, compress_keys)
    comp_values = compress_rows(values[0], following[1], key_position, compress_values)
    every = lax.all_gather(jnp.stack([comp_keys, comp_values], 0), SEQ, axis=1, tiled=True)
    heads = keys.shape[2] // HEAD_DIM
    blocks = every.shape[1]
    all_keys = every[0].reshape(blocks, heads, HEAD_DIM)
    all_values = every[1].reshape(blocks, heads, HEAD_DIM)
    group = queries.shape[2] // HEAD_DIM // heads
    query = queries[0].reshape(qcount, heads, group, HEAD_DIM)
    scores = jnp.einsum("qhgd,bhd->qhgb", query, all_keys, preferred_element_type=jnp.float32) * (
        1.0 / math.sqrt(HEAD_DIM)
    )
    index = seq_pos * qcount + jnp.arange(qcount, dtype=jnp.int32)
    limit = index * skip // STRIDE
    visible = (jnp.arange(blocks, dtype=jnp.int32)[None, :] <= limit[:, None])[:, None, None, :]
    scores = jnp.where(visible, scores, -1e30)
    peak = jnp.max(scores, -1, keepdims=True)
    weights = jnp.where(visible, jnp.exp(scores - peak), 0.0)
    probs = (weights / jnp.sum(weights, -1, keepdims=True)).astype(jnp.bfloat16)
    attended = jnp.einsum("qhgb,bhd->qhgd", probs, all_values, preferred_element_type=jnp.float32)
    attended = attended.astype(jnp.bfloat16).reshape(qcount, heads * group * HEAD_DIM)
    spots = jnp.arange(scored, dtype=jnp.int32) * skip + BLOCK - 1
    valid = (spots[None, :] < lengths[:, None]).astype(jnp.float32)
    count = jnp.sum(valid)
    rows_grp = collect(attended, SEQ, 0)
    part = jnp.dot(rows_grp, out_proj, preferred_element_type=jnp.float32)
    summed = taken_together(part, "mp")
    local_res = residual[batch_pos]
    hidden = (local_res.astype(jnp.float32) + summed).astype(jnp.bfloat16)
    whole = collect(hidden, SEQ, 1)
    normed = normalize(whole, norm_gain)
    logits = vocab_logits(normed, lax.all_gather(lm_head, "batch", axis=0, tiled=True))
    wanted = targets[batch_pos]
    offset = lax.axis_index(SEQ_MP) * lm_head.shape[0] * batch_count
    picked = picked_logit(logits, offset, wanted)
    local_top = jnp.max(logits, 1)
    local_sum = jnp.sum(jnp.exp(logits - local_top[:, None]), 1)
    top, total, target_logit = combined_by_axis((local_top, local_sum, picked), SEQ_MP, join_terms)
    logprob = target_logit - (top + jnp.log(total))
    token_logprob = lax.dynamic_slice_in_dim(logprob, seq_pos * qcount, qcount, 0)[None, :]
    rollout_score = (jnp.sum(valid[batch_pos] * logprob) / count)[None]
    return (token_logprob, rollout_score)


def solution(mesh):
    split = Mesh(
        mesh.devices.reshape(16, 2, mesh.shape["mp"], mesh.shape["batch"]),
        ("seq_0", "seq_1", "mp", "batch"),
    )
    in_specs = (
        P("batch", SEQ, "mp"),
        P("batch", SEQ, "mp"),
        P("batch", SEQ, "mp"),
        P(),
        P(),
        P(),
        P("mp", SEQ),
        P(None, None, SEQ),
        P(),
        P(SEQ_MP_BATCH, None),
        P(),
        P(),
    )
    out_specs = (P("batch", SEQ), P("batch"))
    return jax.shard_map(body, mesh=split, in_specs=in_specs, out_specs=out_specs, check_vma=False)
```

profile of v0, /device:TPU:1, one launch (start us, length us, event | category | flops | bytes accessed | tf_op | source)
XLA Modules:
  0.0 213.9 jit_solution(8704748999628346263)
XLA Ops:
  7.2 0.0 copy-start
  7.2 0.0 copy-start.2
  7.2 0.0 copy-start.3
  7.2 0.0 all-gather.8.cloned.1.call-start
  7.3 0.7 all-gather.8.cloned.1.call-update
  8.0 0.2 copy-done.2
  8.2 8.9 %collective-permute-start = (bf16[16,256]{1,0:T(8,128)(2,1)S(1)}, bf16[16,256]{1,0:T(8,128)(2,1)S(1)}, u32[]{:S(2)}, u32[]{:S(2)}) collective-permute-start(bf16[16,256]{1,0:T(8,128)(2,1)S(1)} %slice_bitcast_fusion.1), channel_id=1, source_target_pairs={{16,0},{32,16},{48,32},{64,48},{80,64},{96,80},{112,96},{128,112},... | collective-permute-start | bytes 24584 | tf_op jit(solution)/shard_map/ppermute | solution.py:20
  17.1 1.9 collective-permute-start.1
  19.0 0.1 iota_compare_fusion
  19.2 0.1 copy.45
  19.2 0.1 copy.48
  19.3 0.0 collective-permute-done
  19.4 0.1 copy.46
  19.5 0.3 fusion.8
  19.8 2.3 %collective-permute-done.1 = bf16[16,256]{1,0:T(8,128)(2,1)S(1)} collective-permute-done((bf16[16,256]{1,0:T(8,128)(2,1)S(1)}, bf16[16,256]{1,0:T(8,128)(2,1)S(1)}, u32[]{:S(2)}, u32[]{:S(2)}) %collective-permute-start.1) | collective-permute-done | bytes 8224 | tf_op jit(solution)/shard_map/ppermute | solution.py:20
  22.1 0.1 copy.49
  22.2 0.3 fusion.9
  22.5 31.6 %all_gather.24 = bf16[2,512,256]{2,1,0:T(8,128)(2,1)S(1)} all-gather(bf16[2,16,256]{2,1,0:T(8,128)(2,1)S(1)} %pad_maximum_fusion.2), channel_id=1, replica_groups=mesh['seq_0'=16,'seq_1'=2,'mp'=4,'batch'=4] {'seq_0','seq_1'}, dimensions={1}, use_global_device_ids=true | all-gather | bytes 540672 | tf_op jit(solution)/shard_map/all_gather | solution.py:131
  54.1 0.1 copy.52
  54.2 0.1 copy.51
  54.4 0.3 fusion.113
  54.7 0.2 fusion.10
  55.0 0.1 broadcast_in_dim.53
  55.1 29.1 %all_to_all.15 = bf16[32,4,1024]{2,1,0:T(4,128)(2,1)S(1)} all-to-all(bf16[32,4,1024]{2,1,0:T(4,128)(2,1)S(1)} %broadcast_in_dim.53), channel_id=1, replica_groups=mesh['seq_0'=16,'seq_1'=2,'mp'=4,'batch'=4] {'seq_0','seq_1'}, dimensions={0} | all-to-all | bytes 524288 | tf_op jit(solution)/shard_map/all_to_all | solution.py:31
  84.2 0.1 reshape.1247
  84.2 0.2 fusion.117
  84.5 0.7 broadcast_in_dim.54
  85.2 4.1 %all-to-all-start.1 = ((f32[4,128,128]{2,1,0:T(8,128)}), f32[4,128,128]{2,1,0:T(8,128)S(1)}, u32[]{:S(2)}, u32[]{:S(2)}) async-start(f32[4,128,128]{2,1,0:T(8,128)} %broadcast_in_dim.54), calls=%async_computation.1 | async-start | bytes 524288 | tf_op jit(solution)/shard_map/all_to_all | solution.py:31
  89.3 5.6 %all-to-all-done.1 = f32[4,128,128]{2,1,0:T(8,128)S(1)} async-done(((f32[4,128,128]{2,1,0:T(8,128)}), f32[4,128,128]{2,1,0:T(8,128)S(1)}, u32[]{:S(2)}, u32[]{:S(2)}) %all-to-all-start.1) | async-done | bytes 262176 | tf_op jit(solution)/shard_map/all_to_all | solution.py:31
  94.9 0.8 fusion.19
  95.7 0.1 copy.57
  95.8 0.0 copy-start.6
  95.8 1.3 broadcast_in_dim.55
  97.2 5.6 %all-to-all-start.2 = ((bf16[32,128,128]{1,2,0:T(8,128)(2,1)}), bf16[32,128,128]{1,2,0:T(8,128)(2,1)S(1)}, u32[]{:S(2)}, u32[]{:S(2)}) async-start(bf16[32,128,128]{1,2,0:T(8,128)(2,1)} %broadcast_in_dim.55), calls=%async_computation.2 | async-start | bytes 2097152 | tf_op jit(solution)/shard_map/all_to_all | solution.py:31
  102.8 0.7 fusion.22
  103.5 0.7 fusion.108
  104.2 0.1 compare_convert_fusion
  104.3 54.3 %all-to-all-done.2 = bf16[32,128,128]{1,2,0:T(8,128)(2,1)S(1)} async-done(((bf16[32,128,128]{1,2,0:T(8,128)(2,1)}), bf16[32,128,128]{1,2,0:T(8,128)(2,1)S(1)}, u32[]{:S(2)}, u32[]{:S(2)}) %all-to-all-start.2) | async-done | bytes 1048608 | tf_op jit(solution)/shard_map/all_to_all | solution.py:31
  158.6 0.6 multiply_reduce_fusion
  159.1 0.7 fusion.2
  159.8 0.0 all-gather.8.cloned.1.call-done
  159.9 6.3 %fusion.114 = (f32[128]{0:T(128)S(1)}, f32[128,1024]{1,0:T(8,128)S(1)}) fusion(bf16[128,4096]{0,1:T(8,128)(2,1)S(1)} %fusion.2, bf16[1024,4096]{1,0:T(8,128)(2,1)} %all-gather.8.cloned.1.call-done), kind=kOutput, calls=%fused_computation.209 | convolution fusion | flops 1073872768 | bytes 9961984 | tf_op jit(solution)/shard_map/dot_general | solution.py:91
  166.2 0.3 exponential_reduce_fusion
  166.5 19.1 %all-gather.3 = f32[16,3,128]{2,1,0:T(4,128)S(1)} all-gather(f32[1,3,128]{2,1,0:T(4,128)S(1)} %maximum_bitcast_fusion), channel_id=2, replica_groups=mesh['seq_0'=16,'seq_1'=2,'mp'=4,'batch'=4] {'seq_0'}, dimensions={0}, use_global_device_ids=true | all-gather | bytes 26112 | tf_op jit(solution)/shard_map/all_gather | solution.py:50
  185.7 9.5 %all-gather.4 = f32[2,3,128]{2,1,0:T(4,128)S(1)} all-gather(f32[1,3,128]{2,1,0:T(4,128)S(1)} %maximum_bitcast_fusion.1), channel_id=3, replica_groups=mesh['seq_0'=16,'seq_1'=2,'mp'=4,'batch'=4] {'seq_1'}, dimensions={0}, use_global_device_ids=true | all-gather | bytes 4608 | tf_op jit(solution)/shard_map/all_gather | solution.py:50
  195.2 8.1 %all-gather.5 = f32[4,3,128]{2,1,0:T(4,128)S(1)} all-gather(f32[1,3,128]{2,1,0:T(4,128)S(1)} %maximum_bitcast_fusion.2), channel_id=4, replica_groups=mesh['seq_0'=16,'seq_1'=2,'mp'=4,'batch'=4] {'mp'}, dimensions={0}, use_global_device_ids=true | all-gather | bytes 7680 | tf_op jit(solution)/shard_map/all_gather | solution.py:50
  203.4 0.6 fusion.25
  204.0 0.6 dynamic-slice_bitcast_fusion
  (42 shorter events, 0.5 us)
Async XLA Ops:
  7.2 12.3 %copy-start = (bf16[4096,128]{1,0:T(8,128)(2,1)S(1)}, bf16[4096,128]{1,0:T(8,128)(2,1)}, u32[]{:S(2)}) copy-start(bf16[4096,128]{1,0:T(8,128)(2,1)} %param.16) | copy-start | bytes 3145732
  7.2 1.0 copy-start.2
  7.2 9.9 %copy-start.3 = (bf16[1,256,256]{2,1,0:T(8,128)(2,1)S(1)}, bf16[1,256,256]{2,1,0:T(8,128)(2,1)}, u32[]{:S(2)}) copy-start(bf16[1,256,256]{2,1,0:T(8,128)(2,1)} %param.14) | copy-start | bytes 393220
  7.2 12.1 %copy-start.7 = (bf16[1,4,1024]{2,1,0:T(4,128)(2,1)S(1)}, bf16[1,4,1024]{2,1,0:T(4,128)(2,1)}, u32[]{:S(2)}) copy-start(bf16[1,4,1024]{2,1,0:T(4,128)(2,1)} %param.12) | copy-start | bytes 24580
  7.2 12.3 %copy-start.5 = (f32[32,128]{1,0:T(8,128)S(1)}, f32[32,128]{1,0:T(8,128)}, u32[]{:S(2)}) copy-start(f32[32,128]{1,0:T(8,128)} %param.15) | copy-start | bytes 49156
  7.2 152.6 %all-gather.8.cloned.1.call-start = ((), (), s32[]{:S(2)}) async-start(), calls=%async_computation.3 | async-start | bytes 10485760 | tf_op jit(solution)/shard_map/all_gather | solution.py:160
  8.2 14.0 %copy-start.1 = (bf16[4096,128]{1,0:T(8,128)(2,1)S(1)}, bf16[4096,128]{1,0:T(8,128)(2,1)}, u32[]{:S(2)}) copy-start(bf16[4096,128]{1,0:T(8,128)(2,1)} %param.17) | copy-start | bytes 3145732
  8.2 11.2 %collective-permute-start = (bf16[16,256]{1,0:T(8,128)(2,1)S(1)}, bf16[16,256]{1,0:T(8,128)(2,1)S(1)}, u32[]{:S(2)}, u32[]{:S(2)}) collective-permute-start(bf16[16,256]{1,0:T(8,128)(2,1)S(1)} %slice_bitcast_fusion.1), channel_id=1, source_target_pairs={{16,0},{32,16},{48,32},{64,48},{80,64},{96,80},{112,96},{128,112},... | collective-permute-start | bytes 24584 | tf_op jit(solution)/shard_map/ppermute | solution.py:20
  17.1 5.0 %collective-permute-start.1 = (bf16[16,256]{1,0:T(8,128)(2,1)S(1)}, bf16[16,256]{1,0:T(8,128)(2,1)S(1)}, u32[]{:S(2)}, u32[]{:S(2)}) collective-permute-start(bf16[16,256]{1,0:T(8,128)(2,1)S(1)} %slice_bitcast_fusion), channel_id=1, source_target_pairs={{16,0},{32,16},{48,32},{64,48},{80,64},{96,80},{112,96},{128,112},... | collective-permute-start | bytes 24584 | tf_op jit(solution)/shard_map/ppermute | solution.py:20
  54.1 30.2 %copy-start.4 = (bf16[1024,128]{1,0:T(8,128)(2,1)S(1)}, bf16[1024,128]{1,0:T(8,128)(2,1)}, u32[]{:S(2)}) copy-start(bf16[1024,128]{1,0:T(8,128)(2,1)} %param.18) | copy-start | bytes 786436
  85.2 18.3 %copy-start.8 = (s32[4]{0:T(128)S(1)}, s32[4]{0:T(128)}, u32[]{:S(2)}) copy-start(s32[4]{0:T(128)} %param.23) | copy-start | bytes 52
  85.2 9.7 %all-to-all-start.1 = ((f32[4,128,128]{2,1,0:T(8,128)}), f32[4,128,128]{2,1,0:T(8,128)S(1)}, u32[]{:S(2)}, u32[]{:S(2)}) async-start(f32[4,128,128]{2,1,0:T(8,128)} %broadcast_in_dim.54), calls=%async_computation.1 | async-start | bytes 524288 | tf_op jit(solution)/shard_map/all_to_all | solution.py:31
  95.8 63.3 %copy-start.6 = (f32[4096]{0:T(1024)S(1)}, f32[4096]{0:T(1024)}, u32[]{:S(2)}) copy-start(f32[4096]{0:T(1024)} %param.20) | copy-start | bytes 49156
  97.2 61.4 %all-to-all-start.2 = ((bf16[32,128,128]{1,2,0:T(8,128)(2,1)}), bf16[32,128,128]{1,2,0:T(8,128)(2,1)S(1)}, u32[]{:S(2)}, u32[]{:S(2)}) async-start(bf16[32,128,128]{1,2,0:T(8,128)(2,1)} %broadcast_in_dim.55), calls=%async_computation.2 | async-start | bytes 2097152 | tf_op jit(solution)/shard_map/all_to_all | solution.py:31
Sparse Core Ops, SparseCore 0:
  10.1 95.8 all-gather.7
where the time goes:
time: 216 us; the launch traced here: 214 us
  blocking collectives  97.4 us (45%)
  waiting for transfers between devices  62.8 us (29%)
  starting transfers between devices  20.6 us (10%)
  between operations  16.8 us (8%)
  matrix products  7.68 us (4%)
  local copies, waits for them, and re-layouts  4.58 us (2%)
  other arithmetic  3.98 us (2%)
    all_to_all x2, waiting for transfers between devices, copy_for_each(): return lax.all_to_all(copies, axis, split_axis=0, concat_axis=0, tiled=True)  59.9 us
    all_gather x3, blocking collectives, all_in_one(): both, at, found = (lax.all_gather(jnp.concatenate(lines), axis), 0, {})  36.8 us
    all_gather x1, blocking collectives, body(): lax.all_gather(jnp.stack([comp_keys, comp_values], 0), SEQ, axis=1, tiled...  31.6 us
    all_to_all x1, blocking collectives, copy_for_each(): return lax.all_to_all(copies, axis, split_axis=0, concat_axis=0, tiled=True)  29.1 us
    ppermute x2, starting transfers between devices, from_behind(): return lax.ppermute(block, axis, route)  10.8 us
    all_to_all x2, starting transfers between devices, copy_for_each(): return lax.all_to_all(copies, axis, split_axis=0, concat_axis=0, tiled=True)  9.76 us
    dot_general x1, matrix products, vocab_logits(): lax.dot_general(normed, rows, (((1,), (1,)), ((), ())), preferred_element...  6.35 us
  transfers between devices with their start and end apart: 5, of which 3 were waited for; matrix products, arithmetic and copies ran while one was open for 4% of the time, Pallas kernels for 0%

commit v1 on v0

v1 whole, which is shorter than its diff:
```python
import functools
import math

import jax
import jax.numpy as jnp
from jax import lax
from jax.experimental import pallas as pl
from jax.experimental.pallas import tpu as pltpu
from jax.sharding import Mesh
from jax.sharding import PartitionSpec as P

BF16 = jnp.bfloat16
F32 = jnp.float32
HEAD_DIM = 128
MESH = pl.DeviceIdType.MESH
AXES = ("seq_0", "seq_1", "mp", "batch")
SEQ = ("seq_0", "seq_1")
SEQ_MP_BATCH = ("seq_0", "seq_1", "mp", "batch")
NZ, NX, NY = 16, 4, 4

SHIFT = (0, 1, 2, -1, -2)
STEP = (0, 5, -5)
OFFSETS = tuple(s + w for s in SHIFT for w in STEP) + (8,)
SLOT_OF = {off % NZ: k for k, off in enumerate(OFFSETS)}
NEAR = (0, 1, -1, 2, -2, 3, -3, 4, -4, 5, -5, 6, -6, 7, -7, 8)
CHUNK = 4
CHUNKS = NZ // CHUNK


def nt_dot(a, b):
    return lax.dot_general(a, b, (((1,), (1,)), ((), ())), preferred_element_type=F32)


def kernel(
    q_ref, k_ref, v_ref, pos_ref, wk_hbm, wv_hbm, op_hbm, res_ref, gain_ref, lm_hbm, tgt_ref, len_ref,
    out_ref,
    w_buf, op_own, op_other, lm_buf, rows_f, xa, xb, pay, epay, bz, kvq, ebuf, qperm, kmat, vmat, att,
    cs, cr, g_own, g_other, rb, normed, acc, st, fr, fs, zr,
    local_sem, b_send, b_recv, a1_send, a1_recv, a2_send, a2_recv, c_send, c_recv, d1_send, d1_recv,
    d2_send, d2_recv, d3_send, d3_recv, d4_send, d4_recv, f1_send, f1_recv, f2_send, f2_recv,
):
    z, c, x, y = (lax.axis_index(name) for name in AXES)
    other = 1 - c

    def at_z(off):
        return lax.rem(z + (off + NZ), NZ)

    def ring4(p, d):
        return lax.rem(p + d, 4)

    barrier = pltpu.get_barrier_semaphore()
    peers = [(at_z(off), core, x, y) for off in range(1, NZ) for core in (0, 1)]
    peers += [(z, other, ring4(x, d), y) for d in range(4)]
    peers += [(z, c, ring4(x, d), ring4(y, e)) for d in range(4) for e in range(4) if d or e]
    for peer in peers:
        pl.semaphore_signal(barrier, inc=1, device_id=peer, device_id_type=MESH)

    loads = [
        pltpu.make_async_copy(wk_hbm, w_buf.at[0], local_sem.at[0]),
        pltpu.make_async_copy(wv_hbm, w_buf.at[1], local_sem.at[1]),
        pltpu.make_async_copy(op_hbm.at[pl.ds(pl.multiple_of(c * 512, 512), 512)], op_own, local_sem.at[2]),
        pltpu.make_async_copy(lm_hbm, lm_buf.at[c], local_sem.at[3]),
    ]
    for load in loads:
        load.start()

    for t, src in enumerate((k_ref, v_ref)):
        for h in range(2):
            rows_f[t, h] = src[0, :, h * 128 : (h + 1) * 128].astype(F32)
    for i in range(16):
        lanes = slice(i * 128, (i + 1) * 128)
        pa, pb = pos_ref[i : i + 1, :], pos_ref[16 + i : 17 + i, :]
        for t in range(2):
            for h in range(2):
                rows = rows_f[t, h, pl.ds(i, 16, stride=16), :]
                xa[t, h * 16 : (h + 1) * 16, lanes] = (rows + pa).astype(BF16)
                xb[t, h * 16 : (h + 1) * 16, lanes] = (rows + pb).astype(BF16)
            xb[t, 32:48, lanes] = jnp.broadcast_to(pb, (16, 128)).astype(BF16)
    qf = q_ref[0].astype(F32)
    for h in range(2):
        lines = [qf[:, (4 * h + g) * 128 : (4 * h + g + 1) * 128] for g in range(4)]
        pay[h, 2] = jnp.concatenate(lines, 0).astype(BF16)
    for t in range(2):
        loads[t].wait()
        first = jnp.dot(xa[t], w_buf[t, :2048], preferred_element_type=F32)
        second = jnp.dot(xb[t], w_buf[t, 2048:], preferred_element_type=F32)
        bz[t] = second[32:33]
        for h in range(2):
            fh, sh = first[h * 16 : (h + 1) * 16], second[h * 16 : (h + 1) * 16]
            pay[h, t] = (fh + pltpu.roll(sh, 15, 0)).astype(BF16)
            epay[h, 2 * t : 2 * t + 1] = fh[15:16]
            epay[h, 2 * t + 1 : 2 * t + 2] = sh[0:1]
    kvq[0, c] = pay[c]
    ebuf[0, c] = epay[c]

    pl.semaphore_wait(barrier, len(peers))

    def remote(src, dst, send, recv, peer):
        return pltpu.make_async_remote_copy(
            src_ref=src, dst_ref=dst, send_sem=send, recv_sem=recv, device_id=peer, device_id_type=MESH
        )

    sent = []

    def go(copy):
        copy.start()
        sent.append(copy)

    def a1(n, k, core, h):
        peer = (at_z(-OFFSETS[k]), core, x, y)
        i = 3 * n + (2 if k == 15 else k - 1) if k else 6
        return (
            remote(pay.at[h], kvq.at[k, c], a1_send.at[2 * i], a1_recv.at[4 * (3 if k == 15 else k) + 2 * c], peer),
            remote(epay.at[h], ebuf.at[k, c], a1_send.at[2 * i + 1], a1_recv.at[4 * (3 if k == 15 else k) + 2 * c + 1], peer),
        )

    for k in (15, 1, 2):
        for n, h in enumerate((c, other)):
            for part in a1(n, k, h, h):
                go(part)
    for part in a1(0, 0, other, other):
        go(part)

    op_copy = remote(op_hbm.at[pl.ds(pl.multiple_of(other * 512, 512), 512)], op_other, b_send.at[0], b_recv.at[0], (z, other, x, y))
    lm_copy = remote(lm_hbm, lm_buf.at[c], b_send.at[1], b_recv.at[1], (z, other, x, y))
    go(op_copy)
    go(lm_copy)

    def a1_arrival(k, core):
        i = 4 * (3 if k == 15 else k) + 2 * core
        remote(pay.at[0], kvq.at[k, core], a1_send.at[0], a1_recv.at[i], (z, c, x, y)).wait_recv()
        remote(epay.at[0], ebuf.at[k, core], a1_send.at[0], a1_recv.at[i + 1], (z, c, x, y)).wait_recv()

    a1_arrival(0, other)
    for k in (1, 2):
        for core in range(2):
            a1_arrival(k, core)

    def a2(g):
        peer = (at_z(-SHIFT[g]), c, x, y)
        return (
            remote(kvq.at[pl.ds(0, 3)], kvq.at[pl.ds(3 * g, 3)], a2_send.at[2 * g - 2], a2_recv.at[2 * g - 2], peer),
            remote(ebuf.at[pl.ds(0, 3)], ebuf.at[pl.ds(3 * g, 3)], a2_send.at[2 * g - 1], a2_recv.at[2 * g - 1], peer),
        )

    for g in (2, 4, 1, 3):
        for part in a2(g):
            go(part)

    col = lax.broadcasted_iota(jnp.int32, (1, 512), 1)
    slot, core_of, lane = col // 32, (col // 16) % 2, col % 16
    g_of, w_of = slot // 3, slot % 3
    off_of = jnp.where(g_of > 2, 2 - g_of, g_of) + jnp.where(w_of == 2, -5, 5 * w_of)
    off_of = jnp.where(slot == 15, 8, off_of)
    seq_of = ((off_of + z + NZ) % NZ) * 2 + core_of
    block_of = seq_of * 16 + lane
    row_of = (lane // 4) * 128 + seq_of * 4 + lane % 4
    perm = jnp.where(lax.broadcasted_iota(jnp.int32, (512, 512), 0) == row_of, 1.0, 0.0).astype(BF16)

    for core in range(2):
        a1_arrival(15, core)
    for g in (1, 3, 2, 4):
        for part in a2(g):
            part.wait_recv()

    q_all = kvq[:, :, 2].reshape(512, 128)
    qperm[...] = jnp.dot(perm, q_all, preferred_element_type=F32).astype(BF16)
    last = lax.broadcasted_iota(jnp.int32, (16, 128), 0) == 15
    for k in range(NZ):
        top = (at_z(OFFSETS[k]) == NZ - 1).astype(F32)
        after = SLOT_OF[(OFFSETS[k] + 1) % NZ]
        for t, mat in enumerate((kmat, vmat)):
            for core in range(2):
                if core == 0:
                    beyond = ebuf[k, 1, 2 * t + 1 : 2 * t + 2]
                else:
                    beyond = ebuf[after, 0, 2 * t + 1 : 2 * t + 2] * (1.0 - top) + bz[t] * top
                fixed = ebuf[k, core, 2 * t : 2 * t + 1] + beyond
                tile = jnp.where(last, fixed, kvq[k, core, t].astype(F32))
                mat[(2 * k + core) * 16 : (2 * k + core + 1) * 16, :] = tile.astype(BF16)

    limit = lax.broadcasted_iota(jnp.int32, (128, 1), 0) * 4
    visible = block_of <= limit
    for g in range(4):
        score = nt_dot(qperm[g * 128 : (g + 1) * 128], kmat[...]) * (1.0 / math.sqrt(HEAD_DIM))
        score = jnp.where(visible, score, -1e30)
        peak = jnp.max(score, -1, keepdims=True)
        weight = jnp.where(visible, jnp.exp(score - peak), 0.0)
        prob = (weight * (1.0 / jnp.sum(weight, -1, keepdims=True))).astype(BF16)
        found = jnp.dot(prob, vmat[...], preferred_element_type=F32)
        att[:, g * 128 : (g + 1) * 128] = found.astype(BF16)

    loads[2].wait()
    cs[0] = jnp.dot(att[...], op_own[...], preferred_element_type=F32).reshape(4, 32, 128)
    op_copy.wait_recv()
    cs[1] = jnp.dot(att[...], op_other[...], preferred_element_type=F32).reshape(4, 32, 128)

    def c_copy(rel, d):
        to = ring4(x, d)
        i = rel * 4 + d
        return remote(cs.at[rel, to], cr.at[i], c_send.at[i], c_recv.at[i], (z, other if rel else c, to, y))

    pairs = [(rel, d) for d in (2, 1, 3, 0) for rel in (0, 1) if rel or d]
    for rel, d in pairs:
        go(c_copy(rel, d))
    total = res_ref[y, pl.ds(pl.multiple_of(32 * x, 32), 32), :].astype(F32)
    summed = cs[0, x]
    for rel, d in reversed(pairs):
        c_copy(rel, d).wait_recv()
        summed = summed + cr[rel * 4 + d]
    p1 = x * other + y * c
    p2 = x * c + y * other
    g_own[p2, p1, 0] = (total + summed).astype(BF16)

    def d1(o):
        return remote(g_own.at[p2, p1, 0], g_own.at[p2, p1, o], d1_send.at[o], d1_recv.at[o], (at_z(-NEAR[o]), c, x, y))

    for o in reversed(range(1, NZ)):
        go(d1(o))

    def along_first(d):
        return (z, c, ring4(x, d * other), ring4(y, d * c))

    def along_second(d):
        return (z, c, ring4(x, d * c), ring4(y, d * other))

    def d2(s, d):
        part = pl.ds(s * CHUNK, CHUNK)
        i = s * 3 + d - 1
        return remote(g_own.at[p2, p1, part], g_own.at[p2, p1, part], d2_send.at[i], d2_recv.at[i], along_first(d))

    def d2_arrival(s, d):
        part = pl.ds(s * CHUNK, CHUNK)
        i = s * 3 + d - 1
        slab = g_own.at[p2, ring4(p1, 4 - d), part]
        remote(slab, slab, d2_send.at[i], d2_recv.at[i], along_first(d)).wait_recv()

    def d3(s, e, d):
        part = pl.ds(s * CHUNK, CHUNK)
        i = (s * 4 + e) * 3 + d - 1
        slab = g_own.at[p2, ring4(p1, 4 - e), part]
        return remote(slab, slab, d3_send.at[i], d3_recv.at[i], along_second(d))

    def d3_arrival(s, e, d):
        part = pl.ds(s * CHUNK, CHUNK)
        i = (s * 4 + e) * 3 + d - 1
        slab = g_own.at[ring4(p2, 4 - d), ring4(p1, 4 - e), part]
        remote(slab, slab, d3_send.at[i], d3_recv.at[i], along_second(d)).wait_recv()

    for s in range(CHUNKS):
        for o in range(max(1, s * CHUNK), (s + 1) * CHUNK):
            d1(o).wait_recv()
        for d in (2, 1, 3):
            go(d2(s, d))
        for d in (2, 1, 3):
            go(d3(s, 0, d))
    for s in range(CHUNKS):
        for e in (1, 3, 2):
            d2_arrival(s, e)
            for d in (2, 1, 3):
                go(d3(s, e, d))
    for s in range(CHUNKS):
        for e in (0, 1, 3, 2):
            for d in (1, 3, 2):
                d3_arrival(s, e, d)

    def held(core_rows, parity, n):
        xx, yy = n % 4, 2 * core_rows + n // 4
        return xx * parity + yy * (1 - parity), xx * (1 - parity) + yy * parity

    def d4(n):
        i, j = held(other, c, n)
        return remote(g_own.at[i, j], g_other.at[i, j], d4_send.at[n], d4_recv.at[n], (z, other, x, y))

    for n in range(8):
        go(d4(n))

    def squares(ref, i, j):
        part = ref[i, j].astype(F32)
        return jnp.sum(part * part, 0)

    for n in range(8):
        i, j = held(c, c, n)
        rb[n] = squares(g_own, i, j)
    for n in range(8):
        i, j = held(c, other, n)
        remote(g_other.at[i, j], g_other.at[i, j], d4_send.at[n], d4_recv.at[n], (z, other, x, y)).wait_recv()
        total_sq = jnp.sum(rb[n] + squares(g_other, i, j), -1, keepdims=True)
        rb[n] = jnp.broadcast_to(lax.rsqrt(total_sq * (1.0 / 4096) + 1e-05), (32, 128))

    loads[3].wait()
    lm_copy_in = remote(lm_hbm, lm_buf.at[other], b_send.at[1], b_recv.at[1], (z, other, x, y))
    lm_copy_in.wait_recv()
    for o in range(NZ):
        for ref, parity in ((g_own, c), (g_other, other)):
            at = pl.multiple_of((at_z(NEAR[o]) * 2 + parity) * 128, 128)
            gain = gain_ref[:, pl.ds(at, 128)]
            for n in range(8):
                i, j = held(c, parity, n)
                normed[n * 32 : (n + 1) * 32, pl.ds(at, 128)] = (ref[i, j, o].astype(F32) * rb[n] * gain).astype(BF16)

    for half in range(2):
        acc[half] = nt_dot(lm_buf[half, :, :512], normed[:, :512])

    @pl.loop(1, 8)
    def _(t):
        lanes = pl.ds(pl.multiple_of(t * 512, 512), 512)
        for half in range(2):
            acc[half] += nt_dot(lm_buf[half, :, lanes], normed[:, lanes])

    logits = [acc[0], acc[1]]
    peak = jnp.maximum(jnp.max(logits[0], 0, keepdims=True), jnp.max(logits[1], 0, keepdims=True))
    wanted = jnp.concatenate([tgt_ref[pl.ds(2 * c, 1), :], tgt_ref[pl.ds(2 * c + 1, 1), :]], 1)
    spread = jnp.zeros((1, 256), F32)
    picked = jnp.zeros((1, 256), F32)
    for half in range(2):
        base = (((2 * z + half) * NX + x) * NY + y) * 256
        entry = base + lax.broadcasted_iota(jnp.int32, (256, 256), 0)
        spread += jnp.sum(jnp.exp(logits[half] - peak), 0, keepdims=True)
        picked += jnp.sum(jnp.where(entry == wanted, logits[half], 0.0), 0, keepdims=True)
    partial = peak + jnp.log(spread)
    for n in range(2):
        st[n, 0:1] = partial[:, n * 128 : (n + 1) * 128]
        st[n, 1:2] = picked[:, n * 128 : (n + 1) * 128]

    active = c == y // 2

    def f1(n, d, e):
        i = d * 4 + e
        return remote(st.at[n], fr.at[x * 4 + y], f1_send.at[n * 4 + d], f1_recv.at[i], (z, c, ring4(x, d), 2 * c + n))

    for n in range(2):
        e = lax.rem(2 * c + n - y + 4, 4)
        for d in (2, 1, 3):
            f1(n, d, e).start()

        @pl.when(e != 0)
        def _():
            f1(n, 0, e).start()

        @pl.when(e == 0)
        def _():
            fr[x * 4 + y] = st[n]

    def joined(ref):
        heads = [ref[n] for n in range(16)]
        high = functools.reduce(jnp.maximum, [part[0:1] for part in heads])
        mass = functools.reduce(jnp.add, [jnp.exp(part[0:1] - high) for part in heads])
        return high + jnp.log(mass), functools.reduce(jnp.add, [part[1:2] for part in heads])

    def f2(o, core, n):
        return remote(fs, zr.at[o], f2_send.at[2 * o + n], f2_recv.at[o], (at_z(-NEAR[o]), core, x, y))

    @pl.when(active)
    def _():
        for d in range(4):
            for e in range(4):
                if d or e:
                    here = fr.at[lax.rem(x + 4 - d, 4) * 4 + lax.rem(y + 4 - e, 4)]
                    remote(st.at[0], here, f1_send.at[0], f1_recv.at[d * 4 + e], (z, c, x, y)).wait_recv()
        level, hit = joined(fr)
        fs[0:1] = level
        fs[1:2] = hit
        for o in reversed(range(1, NZ)):
            f2(o, c, 0).start()
            f2(o, other, 1).start()
        f2(0, other, 1).start()
        zr[0] = fs[...]

    for o in range(1, NZ):
        f2(o, c, 0).wait_recv()

    @pl.when(jnp.logical_not(active))
    def _():
        f2(0, other, 1).wait_recv()

    level, hit = joined(zr)
    logprob = hit - level
    spots = lax.broadcasted_iota(jnp.int32, (1, 128), 1) * 64 + 31
    count = jnp.zeros((1, 1), F32)
    for n in range(4):
        count += jnp.sum(jnp.where(spots < len_ref[n], 1.0, 0.0), -1, keepdims=True)
    mine = jnp.where(spots < len_ref[y], 1.0, 0.0)
    score = jnp.sum(mine * logprob, -1, keepdims=True) / count
    out_ref[0:1] = logprob
    out_ref[1:2] = jnp.broadcast_to(score, (1, 128))

    for copy in sent:
        copy.wait_send()
    for n in range(2):
        e = lax.rem(2 * c + n - y + 4, 4)
        for d in (2, 1, 3):
            f1(n, d, e).wait_send()

        @pl.when(e != 0)
        def _():
            f1(n, 0, e).wait_send()

    @pl.when(active)
    def _():
        for o in reversed(range(1, NZ)):
            f2(o, c, 0).wait_send()
            f2(o, other, 1).wait_send()
        f2(0, other, 1).wait_send()


def body(
    queries, keys, values, key_position, compress_keys, compress_values,
    out_proj, residual, norm_gain, lm_head, targets, lengths,
):
    vmem = pl.BlockSpec(memory_space=pltpu.VMEM)
    hbm = pl.BlockSpec(memory_space=pl.ANY)
    smem = pl.BlockSpec(memory_space=pltpu.SMEM)
    dma = pltpu.SemaphoreType.DMA
    found = pl.pallas_call(
        kernel,
        out_shape=jax.ShapeDtypeStruct((2, 128), F32),
        in_specs=[vmem, vmem, vmem, vmem, hbm, hbm, hbm, vmem, vmem, hbm, vmem, smem],
        out_specs=vmem,
        scratch_shapes=[
            pltpu.VMEM((2, 4096, 128), BF16),
            pltpu.VMEM((512, 128), BF16),
            pltpu.VMEM((512, 128), BF16),
            pltpu.VMEM((2, 256, 4096), BF16),
            pltpu.VMEM((2, 2, 256, 128), F32),
            pltpu.VMEM((2, 32, 2048), BF16),
            pltpu.VMEM((2, 48, 2048), BF16),
            pltpu.VMEM((2, 3, 16, 128), BF16),
            pltpu.VMEM((2, 4, 128), F32),
            pltpu.VMEM((2, 1, 128), F32),
            pltpu.VMEM((16, 2, 3, 16, 128), BF16),
            pltpu.VMEM((16, 2, 4, 128), F32),
            pltpu.VMEM((512, 128), BF16),
            pltpu.VMEM((512, 128), BF16),
            pltpu.VMEM((512, 128), BF16),
            pltpu.VMEM((128, 512), BF16),
            pltpu.VMEM((2, 4, 32, 128), F32),
            pltpu.VMEM((8, 32, 128), F32),
            pltpu.VMEM((4, 4, 16, 32, 128), BF16),
            pltpu.VMEM((4, 4, 16, 32, 128), BF16),
            pltpu.VMEM((8, 32, 128), F32),
            pltpu.VMEM((256, 4096), BF16),
            pltpu.VMEM((2, 256, 256), F32),
            pltpu.VMEM((2, 2, 128), F32),
            pltpu.VMEM((16, 2, 128), F32),
            pltpu.VMEM((2, 128), F32),
            pltpu.VMEM((16, 2, 128), F32),
            dma((4,)),
            dma((2,)), dma((2,)),
            dma((14,)), dma((16,)),
            dma((8,)), dma((8,)),
            dma((8,)), dma((8,)),
            dma((16,)), dma((16,)),
            dma((12,)), dma((12,)),
            dma((48,)), dma((48,)),
            dma((8,)), dma((8,)),
            dma((8,)), dma((16,)),
            dma((32,)), dma((16,)),
        ],
        compiler_params=pltpu.CompilerParams(
            collective_id=0, has_side_effects=True, vmem_limit_bytes=48 * 1024 * 1024
        ),
    )(
        queries, keys, values, key_position, compress_keys, compress_values,
        out_proj, residual, norm_gain.reshape(1, -1), lm_head, targets, lengths,
    )
    seq_pos = lax.axis_index(SEQ)
    token_logprob = lax.dynamic_slice(found, (0, seq_pos * 4), (1, 4))
    return token_logprob, found[1, :1]


def solution(mesh):
    split = Mesh(
        mesh.devices.reshape(16, 2, mesh.shape["mp"], mesh.shape["batch"]),
        ("seq_0", "seq_1", "mp", "batch"),
    )
    in_specs = (
        P("batch", SEQ, "mp"),
        P("batch", SEQ, "mp"),
        P("batch", SEQ, "mp"),
        P(),
        P(),
        P(),
        P("mp", SEQ),
        P(None, None, SEQ),
        P(),
        P(SEQ_MP_BATCH, None),
        P(),
        P(),
    )
    out_specs = (P("batch", SEQ), P("batch"))
    return jax.shard_map(body, mesh=split, in_specs=in_specs, out_specs=out_specs, check_vma=False)
```

time: 216 us -> 99.5 us (0.46)
  blocking collectives: 97.4 us -> 0 us
  Pallas kernels: 0 us -> 86.1 us
  waiting for transfers between devices: 62.8 us -> 0 us
  starting transfers between devices: 20.6 us -> 0 us
  between operations: 16.8 us -> 0.67 us
  local copies, waits for them, and re-layouts: 4.58 us -> 12.3 us
  matrix products: 7.68 us -> 0 us
  other arithmetic: 3.98 us -> 0 us
    pallas_call x0 -> x1, Pallas kernels: none -> 86.1 us  [body(): pl.pallas_call(kernel, out_shape=jax.ShapeDtypeStruct((2, 128), F32), in_...]
    all_gather x4 -> x0, blocking collectives: 68.3 us -> none  [the longest x3 36.8 us: all_in_one(): both, at, found = (lax.all_gather(jnp.concatenate(lines), axis), 0, {})]
    all_to_all x2 -> x0, waiting for transfers between devices: 59.9 us -> none  [copy_for_each(): return lax.all_to_all(copies, axis, split_axis=0, concat_axis=0, tiled=True)]
    all_to_all x1 -> x0, blocking collectives: 29.1 us -> none  [copy_for_each(): return lax.all_to_all(copies, axis, split_axis=0, concat_axis=0, tiled=True)]
    unnamed x18 -> x24, local copies, waits for them, and re-layouts: 0.26 us -> 11.2 us
    ppermute x2 -> x0, starting transfers between devices: 10.8 us -> none  [from_behind(): return lax.ppermute(block, axis, route)]
    all_to_all x2 -> x0, starting transfers between devices: 9.76 us -> none  [copy_for_each(): return lax.all_to_all(copies, axis, split_axis=0, concat_axis=0, tiled=True)]
    dot_general x5 -> x0, matrix products: 7.34 us -> none  [the longest x1 6.35 us: vocab_logits(): lax.dot_general(normed, rows, (((1,), (1,)), ((), ())), preferred_element...]
  transfers between devices with their start and end apart: 5 -> 0, of which waited for: 3 -> 0; matrix products, arithmetic and copies ran while one was open for 4% -> 0% of each run, Pallas kernels for 0% -> 0%
where the time goes in v1:
time: 99.5 us; the launch traced here: 99 us
  Pallas kernels  86.1 us (87%)
  local copies, waits for them, and re-layouts  12.3 us (12%)
    pallas_call x1, Pallas kernels, body(): pl.pallas_call(kernel, out_shape=jax.ShapeDtypeStruct((2, 128), F32), in_...  86.1 us
    unnamed x24, local copies, waits for them, and re-layouts  11.2 us

profile of v1, /device:TPU:1, one launch (start us, length us, event | category | flops | bytes accessed | tf_op | source)
XLA Modules:
  0.0 99.0 jit_solution(5445624317129237084)
XLA Ops:
  0.6 0.0 copy-start
  0.7 1.6 %copy-done = bf16[256,4096]{1,0:T(8,128)(2,1)S(1)} copy-done((bf16[256,4096]{1,0:T(8,128)(2,1)S(1)}, bf16[256,4096]{1,0:T(8,128)(2,1)}, u32[]{:S(2)}) %copy-start) | copy-done | bytes 2097176
  2.2 0.0 copy-start.1
  2.2 1.2 %copy-done.1 = bf16[4096,128]{1,0:T(8,128)(2,1)S(1)} copy-done((bf16[4096,128]{1,0:T(8,128)(2,1)S(1)}, bf16[4096,128]{1,0:T(8,128)(2,1)}, u32[]{:S(2)}) %copy-start.1) | copy-done | bytes 1048600
  3.5 0.0 copy-start.2
  3.5 1.2 %copy-done.2 = bf16[4096,128]{1,0:T(8,128)(2,1)S(1)} copy-done((bf16[4096,128]{1,0:T(8,128)(2,1)S(1)}, bf16[4096,128]{1,0:T(8,128)(2,1)}, u32[]{:S(2)}) %copy-start.2) | copy-done | bytes 1048600
  4.7 0.0 copy-start.3
  4.7 0.9 copy-done.3
  5.6 0.0 copy-start.4
  5.6 0.9 copy-done.4
  6.5 0.0 copy-start.5
  6.5 0.9 copy-done.5
  7.4 0.0 copy-start.6
  7.4 0.9 copy-done.6
  8.3 0.0 copy-start.7
  8.4 0.7 copy-done.7
  9.1 0.0 copy-start.8
  9.1 0.7 copy-done.8
  9.8 0.0 copy-start.9
  9.8 0.7 copy-done.9
  10.5 0.0 copy-start.10
  10.5 0.7 copy-done.10
  11.2 0.0 copy-start.11
  11.2 0.7 copy-done.11
  11.8 86.1 %shard_map.131 = f32[2,128]{1,0:T(2,128)S(1)} custom-call(bf16[1,4,1024]{2,1,0:T(4,128)(2,1)S(1)} %copy-done.9, bf16[1,256,256]{2,1,0:T(8,128)(2,1)S(1)} %copy-done.4, bf16[1,256,256]{2,1,0:T(8,128)(2,1)S(1)} %copy-done.5, f32[32,128]{1,0:T(8,128)S(1)} %copy-done.7, bf16[4096,128]{1,0:T(8,128)(2,1)S(1)} %copy-done.1, bf16[4096,128]{1,0:T(8,128)(2,1)S(1)} %copy-done.2, ...), custom_call_target="tpu_custom_call" | custom-call | tf_op jit(solution)/shard_map/pallas_call | solution.py:415
  97.9 0.6 constant_dynamic-slice_fusion
  98.5 0.5 slice.3
Async XLA Ops:
  0.6 1.6 %copy-start = (bf16[256,4096]{1,0:T(8,128)(2,1)S(1)}, bf16[256,4096]{1,0:T(8,128)(2,1)}, u32[]{:S(2)}) copy-start(bf16[256,4096]{1,0:T(8,128)(2,1)} %lm_hbm.1) | copy-start | bytes 6291460
  2.2 1.2 %copy-start.1 = (bf16[4096,128]{1,0:T(8,128)(2,1)S(1)}, bf16[4096,128]{1,0:T(8,128)(2,1)}, u32[]{:S(2)}) copy-start(bf16[4096,128]{1,0:T(8,128)(2,1)} %wk_hbm.1) | copy-start | bytes 3145732
  3.5 1.2 %copy-start.2 = (bf16[4096,128]{1,0:T(8,128)(2,1)S(1)}, bf16[4096,128]{1,0:T(8,128)(2,1)}, u32[]{:S(2)}) copy-start(bf16[4096,128]{1,0:T(8,128)(2,1)} %wv_hbm.1) | copy-start | bytes 3145732
  4.7 0.9 copy-start.3
  5.6 0.9 copy-start.4
  6.5 0.9 copy-start.5
  7.4 0.9 copy-start.6
  8.3 0.7 copy-start.7
  9.1 0.7 copy-start.8
  9.8 0.7 copy-start.9
  10.5 0.7 copy-start.10
  11.2 0.7 copy-start.11

commit v2 on v1

--- a/solution.py
+++ b/solution.py
@@ -32,11 +32,11 @@
 
 
 def kernel(
-    q_ref, k_ref, v_ref, pos_ref, wk_hbm, wv_hbm, op_hbm, res_ref, gain_ref, lm_hbm, tgt_ref, len_ref,
+    q_hbm, k_hbm, v_hbm, pos_hbm, wk_hbm, wv_hbm, op_hbm, res_hbm, gain_hbm, lm_hbm, tgt_hbm, len_hbm,
     out_ref,
-    w_buf, op_own, op_other, lm_buf, rows_f, xa, xb, pay, epay, bz, kvq, ebuf, qperm, kmat, vmat, att,
+    q_ref, k_ref, v_ref, pos_ref, res_ref, gain_ref, tgt_ref, len_ref, w_buf, op_own, op_other, lm_buf, rows_f, xa, xb, pay, epay, bz, kvq, ebuf, qperm, kmat, vmat, att,
     cs, cr, g_own, g_other, rb, normed, acc, st, fr, fs, zr,
-    local_sem, b_send, b_recv, a1_send, a1_recv, a2_send, a2_recv, c_send, c_recv, d1_send, d1_recv,
+    local_sem, small_sem, b_send, b_recv, a1_send, a1_recv, a2_send, a2_recv, c_send, c_recv, d1_send, d1_recv,
     d2_send, d2_recv, d3_send, d3_recv, d4_send, d4_recv, f1_send, f1_recv, f2_send, f2_recv,
 ):
     z, c, x, y = (lax.axis_index(name) for name in AXES)
@@ -61,8 +61,17 @@
         pltpu.make_async_copy(op_hbm.at[pl.ds(pl.multiple_of(c * 512, 512), 512)], op_own, local_sem.at[2]),
         pltpu.make_async_copy(lm_hbm, lm_buf.at[c], local_sem.at[3]),
     ]
-    for load in loads:
+    small = [
+        pltpu.make_async_copy(src, dst, small_sem.at[n])
+        for n, (src, dst) in enumerate((
+            (k_hbm, k_ref), (v_hbm, v_ref), (pos_hbm, pos_ref), (q_hbm, q_ref),
+            (res_hbm, res_ref), (gain_hbm, gain_ref), (tgt_hbm, tgt_ref), (len_hbm, len_ref),
+        ))
+    ]
+    for load in small[:4] + loads + small[4:]:
         load.start()
+    for load in small[:4]:
+        load.wait()
 
     for t, src in enumerate((k_ref, v_ref)):
         for h in range(2):
@@ -203,6 +212,8 @@
     pairs = [(rel, d) for d in (2, 1, 3, 0) for rel in (0, 1) if rel or d]
     for rel, d in pairs:
         go(c_copy(rel, d))
+    for load in small[4:]:
+        load.wait()
     total = res_ref[y, pl.ds(pl.multiple_of(32 * x, 32), 32), :].astype(F32)
     summed = cs[0, x]
     for rel, d in reversed(pairs):
@@ -409,15 +420,22 @@
     out_proj, residual, norm_gain, lm_head, targets, lengths,
 ):
     vmem = pl.BlockSpec(memory_space=pltpu.VMEM)
-    hbm = pl.BlockSpec(memory_space=pl.ANY)
-    smem = pl.BlockSpec(memory_space=pltpu.SMEM)
+    hbm = pl.BlockSpec(memory_space=pltpu.HBM)
     dma = pltpu.SemaphoreType.DMA
     found = pl.pallas_call(
         kernel,
         out_shape=jax.ShapeDtypeStruct((2, 128), F32),
-        in_specs=[vmem, vmem, vmem, vmem, hbm, hbm, hbm, vmem, vmem, hbm, vmem, smem],
+        in_specs=[hbm] * 12,
         out_specs=vmem,
         scratch_shapes=[
+            pltpu.VMEM((1, 4, 1024), BF16),
+            pltpu.VMEM((1, 256, 256), BF16),
+            pltpu.VMEM((1, 256, 256), BF16),
+            pltpu.VMEM((32, 128), F32),
+            pltpu.VMEM((4, 128, 128), BF16),
+            pltpu.VMEM((1, 4096), F32),
+            pltpu.VMEM((4, 128), jnp.int32),
+            pltpu.SMEM((4,), jnp.int32),
             pltpu.VMEM((2, 4096, 128), BF16),
             pltpu.VMEM((512, 128), BF16),
             pltpu.VMEM((512, 128), BF16),
@@ -445,7 +463,7 @@
             pltpu.VMEM((16, 2, 128), F32),
             pltpu.VMEM((2, 128), F32),
             pltpu.VMEM((16, 2, 128), F32),
-            dma((4,)),
+            dma((4,)), dma((8,)),
             dma((2,)), dma((2,)),
             dma((14,)), dma((16,)),
             dma((8,)), dma((8,)),
@@ -458,7 +476,7 @@
             dma((32,)), dma((16,)),
         ],
         compiler_params=pltpu.CompilerParams(
-            collective_id=0, has_side_effects=True, vmem_limit_bytes=48 * 1024 * 1024
+            collective_id=0, has_side_effects=True, vmem_limit_bytes=67043328
         ),
     )(
         queries, keys, values, key_position, compress_keys, compress_values,

time: 99.5 us -> 89.5 us (0.90)
  local copies, waits for them, and re-layouts: 12.3 us -> 2.46 us
    unnamed x24 -> x0, local copies, waits for them, and re-layouts: 11.2 us -> none
where the time goes in v2:
time: 89.5 us; the launch traced here: 89.3 us
  Pallas kernels  86.2 us (96%)
  local copies, waits for them, and re-layouts  2.46 us (3%)
    pallas_call x1, Pallas kernels, body(): pl.pallas_call(kernel, out_shape=jax.ShapeDtypeStruct((2, 128), F32), in_...  86.2 us

profile of v2, /device:TPU:1, one launch (start us, length us, event | category | flops | bytes accessed | tf_op | source)
XLA Modules:
  0.0 89.3 jit_solution(16622669456894222536)
XLA Ops:
  0.6 86.2 %shard_map.131 = f32[2,128]{1,0:T(2,128)} custom-call(bf16[1,4,1024]{2,1,0:T(4,128)(2,1)} %q_hbm.1, bf16[1,256,256]{2,1,0:T(8,128)(2,1)} %k_hbm.1, bf16[1,256,256]{2,1,0:T(8,128)(2,1)} %v_hbm.1, f32[32,128]{1,0:T(8,128)} %pos_hbm.1, bf16[4096,128]{1,0:T(8,128)(2,1)} %wk_hbm.1, bf16[4096,128]{1,0:T(8,128)(2,1)} %wv_hbm.1, bf16[1024,128]{1,0:T(8,128)(2,1)} %op_hbm.1, ...), custom_call_target="tpu_custom_call" | custom-call | tf_op jit(solution)/shard_map/pallas_call | solution.py:425
  86.9 1.3 %constant_dynamic-slice_fusion = f32[1,4]{1,0:T(1,128)} fusion(f32[2,128]{1,0:T(2,128)} %shard_map.131, s32[]{:T(128)S(6)} %select_n.3), kind=kLoop, calls=%fused_computation | loop fusion | bytes 36 | tf_op jit(solution)/shard_map/dynamic_slice | solution.py:486
  88.1 1.2 %slice.3 = f32[1,1]{1,0:T(1,128)} slice(f32[2,128]{1,0:T(2,128)} %shard_map.131), slice={[1:2], [0:1]} | slice | bytes 8 | tf_op jit(solution)/shard_map/slice | solution.py:487

commit v3 on v2

--- a/solution.py
+++ b/solution.py
@@ -21,10 +21,12 @@
 SHIFT = (0, 1, 2, -1, -2)
 STEP = (0, 5, -5)
 OFFSETS = tuple(s + w for s in SHIFT for w in STEP) + (8,)
+ROUND_ONE = (1, 2, 6, 12, 3, 9, 0)
 SLOT_OF = {off % NZ: k for k, off in enumerate(OFFSETS)}
 NEAR = (0, 1, -1, 2, -2, 3, -3, 4, -4, 5, -5, 6, -6, 7, -7, 8)
 CHUNK = 4
 CHUNKS = NZ // CHUNK
+LAST = CHUNKS - 1
 
 
 def nt_dot(a, b):
@@ -117,13 +119,13 @@
 
     def a1(n, k, core, h):
         peer = (at_z(-OFFSETS[k]), core, x, y)
-        i = 3 * n + (2 if k == 15 else k - 1) if k else 6
+        i, j = 4 * ROUND_ONE.index(k) + 2 * n, 4 * ROUND_ONE.index(k) + 2 * c
         return (
-            remote(pay.at[h], kvq.at[k, c], a1_send.at[2 * i], a1_recv.at[4 * (3 if k == 15 else k) + 2 * c], peer),
-            remote(epay.at[h], ebuf.at[k, c], a1_send.at[2 * i + 1], a1_recv.at[4 * (3 if k == 15 else k) + 2 * c + 1], peer),
+            remote(pay.at[h], kvq.at[k, c], a1_send.at[i], a1_recv.at[j], peer),
+            remote(epay.at[h], ebuf.at[k, c], a1_send.at[i + 1], a1_recv.at[j + 1], peer),
         )
 
-    for k in (15, 1, 2):
+    for k in ROUND_ONE[:-1]:
         for n, h in enumerate((c, other)):
             for part in a1(n, k, h, h):
                 go(part)
@@ -136,22 +138,33 @@
     go(lm_copy)
 
     def a1_arrival(k, core):
-        i = 4 * (3 if k == 15 else k) + 2 * core
-        remote(pay.at[0], kvq.at[k, core], a1_send.at[0], a1_recv.at[i], (z, c, x, y)).wait_recv()
-        remote(epay.at[0], ebuf.at[k, core], a1_send.at[0], a1_recv.at[i + 1], (z, c, x, y)).wait_recv()
-
-    a1_arrival(0, other)
+        j = 4 * ROUND_ONE.index(k) + 2 * core
+        remote(pay.at[0], kvq.at[k, core], a1_send.at[0], a1_recv.at[j], (z, c, x, y)).wait_recv()
+        remote(epay.at[0], ebuf.at[k, core], a1_send.at[0], a1_recv.at[j + 1], (z, c, x, y)).wait_recv()
+
     for k in (1, 2):
         for core in range(2):
             a1_arrival(k, core)
 
     def a2(g):
         peer = (at_z(-SHIFT[g]), c, x, y)
+        src, dst, i = pl.ds(1, 2), pl.ds(3 * g + 1, 2), 2 * g - 2
         return (
-            remote(kvq.at[pl.ds(0, 3)], kvq.at[pl.ds(3 * g, 3)], a2_send.at[2 * g - 2], a2_recv.at[2 * g - 2], peer),
-            remote(ebuf.at[pl.ds(0, 3)], ebuf.at[pl.ds(3 * g, 3)], a2_send.at[2 * g - 1], a2_recv.at[2 * g - 1], peer),
+            remote(kvq.at[src], kvq.at[dst], a2_send.at[i], a2_recv.at[i], peer),
+            remote(ebuf.at[src], ebuf.at[dst], a2_send.at[i + 1], a2_recv.at[i + 1], peer),
         )
 
+    def a2_far(n):
+        peer = (at_z(-3 if n == 0 else 3), c, x, y)
+        i = 8 + 2 * n
+        return (
+            remote(kvq.at[1 + n, n], kvq.at[15, n], a2_send.at[i], a2_recv.at[i], peer),
+            remote(ebuf.at[1 + n, n], ebuf.at[15, n], a2_send.at[i + 1], a2_recv.at[i + 1], peer),
+        )
+
+    for n in (0, 1):
+        for part in a2_far(n):
+            go(part)
     for g in (2, 4, 1, 3):
         for part in a2(g):
             go(part)
@@ -166,10 +179,15 @@
     row_of = (lane // 4) * 128 + seq_of * 4 + lane % 4
     perm = jnp.where(lax.broadcasted_iota(jnp.int32, (512, 512), 0) == row_of, 1.0, 0.0).astype(BF16)
 
-    for core in range(2):
-        a1_arrival(15, core)
+    a1_arrival(0, other)
+    for k in (3, 9, 6, 12):
+        for core in range(2):
+            a1_arrival(k, core)
     for g in (1, 3, 2, 4):
         for part in a2(g):
+            part.wait_recv()
+    for n in (0, 1):
+        for part in a2_far(n):
             part.wait_recv()
 
     q_all = kvq[:, :, 2].reshape(512, 128)
@@ -235,68 +253,105 @@
     def along_second(d):
         return (z, c, ring4(x, d * c), ring4(y, d * other))
 
-    def d2(s, d):
-        part = pl.ds(s * CHUNK, CHUNK)
-        i = s * 3 + d - 1
-        return remote(g_own.at[p2, p1, part], g_own.at[p2, p1, part], d2_send.at[i], d2_recv.at[i], along_first(d))
-
-    def d2_arrival(s, d):
-        part = pl.ds(s * CHUNK, CHUNK)
-        i = s * 3 + d - 1
-        slab = g_own.at[p2, ring4(p1, 4 - d), part]
-        remote(slab, slab, d2_send.at[i], d2_recv.at[i], along_first(d)).wait_recv()
-
-    def d3(s, e, d):
-        part = pl.ds(s * CHUNK, CHUNK)
-        i = (s * 4 + e) * 3 + d - 1
-        slab = g_own.at[p2, ring4(p1, 4 - e), part]
+    SIDE = {1: 0, 3: 1, 2: 2}
+
+    def whole(s):
+        return pl.ds(s * CHUNK, CHUNK)
+
+    def half(s, n):
+        return pl.ds(s * CHUNK + n * (CHUNK // 2), CHUNK // 2)
+
+    def first(slab, i, d):
+        return remote(slab, slab, d2_send.at[i], d2_recv.at[i], along_first(d))
+
+    def second(slab, i, d):
         return remote(slab, slab, d3_send.at[i], d3_recv.at[i], along_second(d))
 
-    def d3_arrival(s, e, d):
-        part = pl.ds(s * CHUNK, CHUNK)
-        i = (s * 4 + e) * 3 + d - 1
-        slab = g_own.at[ring4(p2, 4 - d), ring4(p1, 4 - e), part]
-        remote(slab, slab, d3_send.at[i], d3_recv.at[i], along_second(d)).wait_recv()
-
-    for s in range(CHUNKS):
+    def slab1(e, part):
+        return g_own.at[p2, ring4(p1, (4 - e) % 4), part]
+
+    def slab2(d, e, part):
+        return g_own.at[ring4(p2, (4 - d) % 4), ring4(p1, (4 - e) % 4), part]
+
+    def send_first(s):
+        for d in (2, 1, 3) if s == LAST else (1, 3):
+            go(first(slab1(0, whole(s)), s * 4 + SIDE[d], d))
+
+    def send_second(s, e):
+        for d in (2, 1, 3) if s == LAST else (1, 3):
+            go(second(slab1(e, whole(s)), (s * 4 + e) * 4 + SIDE[d], d))
+
+    def on_first(s, e):
+        if e == 2 and s < LAST:
+            for n in range(2):
+                first(slab1(2, half(s, n)), s * 4 + 2 + n, 1).wait_recv()
+        else:
+            first(slab1(e, whole(s)), s * 4 + SIDE[e], 1).wait_recv()
+            if s < LAST:
+                go(first(slab1(e, half(s, SIDE[e])), s * 4 + 2 + SIDE[e], e))
+        send_second(s, e)
+
+    def on_second(s, e, d):
+        base = (s * 4 + e) * 4
+        if d == 2 and s < LAST:
+            for n in range(2):
+                second(slab2(2, e, half(s, n)), base + 2 + n, 1).wait_recv()
+        else:
+            second(slab2(d, e, whole(s)), base + SIDE[d], 1).wait_recv()
+            if s < LAST:
+                go(second(slab2(d, e, half(s, SIDE[d])), base + 2 + SIDE[d], d))
+
+    def on_origin(s):
         for o in range(max(1, s * CHUNK), (s + 1) * CHUNK):
             d1(o).wait_recv()
-        for d in (2, 1, 3):
-            go(d2(s, d))
-        for d in (2, 1, 3):
-            go(d3(s, 0, d))
-    for s in range(CHUNKS):
-        for e in (1, 3, 2):
-            d2_arrival(s, e)
-            for d in (2, 1, 3):
-                go(d3(s, e, d))
-    for s in range(CHUNKS):
-        for e in (0, 1, 3, 2):
-            for d in (1, 3, 2):
-                d3_arrival(s, e, d)
+        send_first(s)
+        send_second(s, 0)
 
     def held(core_rows, parity, n):
         xx, yy = n % 4, 2 * core_rows + n // 4
         return xx * parity + yy * (1 - parity), xx * (1 - parity) + yy * parity
 
-    def d4(n):
-        i, j = held(other, c, n)
-        return remote(g_own.at[i, j], g_other.at[i, j], d4_send.at[n], d4_recv.at[n], (z, other, x, y))
-
+    def d4(s, n, rows, parity, src, dst):
+        i, j = held(rows, parity, n)
+        k = s * 8 + n
+        return remote(src.at[i, j, whole(s)], dst.at[i, j, whole(s)], d4_send.at[k], d4_recv.at[k], (z, other, x, y))
+
+    def squares(ref, s, rows, parity, n):
+        i, j = held(rows, parity, n)
+        part = ref[i, j, s * CHUNK : (s + 1) * CHUNK].astype(F32)
+        return jnp.sum(part * part, 0)
+
+    def on_complete(s):
+        for n in range(8):
+            go(d4(s, n, other, c, g_own, g_other))
+        for n in range(8):
+            found = squares(g_own, s, c, c, n)
+            rb[n] = found if s == 0 else rb[n] + found
+
+    events = []
+    for s in range(CHUNKS):
+        start = 3.0 + 2.0 * s
+        twice = 3.5 if s == LAST else 5.6
+        events.append((start, s, 0, functools.partial(on_origin, s)))
+        latest = start
+        for e in (0, 1, 3, 2):
+            ready = start + (0.0, 2.8, twice, 2.8)[e]
+            if e:
+                events.append((ready, s, 1, functools.partial(on_first, s, e)))
+            for d in (1, 3, 2):
+                arrival = ready + (0.0, 2.8, twice, 2.8)[d]
+                latest = max(latest, arrival)
+                events.append((arrival, s, 2, functools.partial(on_second, s, e, d)))
+        events.append((latest, s, 3, functools.partial(on_complete, s)))
+    for event in sorted(events, key=lambda item: item[:3]):
+        event[3]()
+
+    for s in range(CHUNKS):
+        for n in range(8):
+            d4(s, n, c, other, g_other, g_other).wait_recv()
+            rb[n] = rb[n] + squares(g_other, s, c, other, n)
     for n in range(8):
-        go(d4(n))
-
-    def squares(ref, i, j):
-        part = ref[i, j].astype(F32)
-        return jnp.sum(part * part, 0)
-
-    for n in range(8):
-        i, j = held(c, c, n)
-        rb[n] = squares(g_own, i, j)
-    for n in range(8):
-        i, j = held(c, other, n)
-        remote(g_other.at[i, j], g_other.at[i, j], d4_send.at[n], d4_recv.at[n], (z, other, x, y)).wait_recv()
-        total_sq = jnp.sum(rb[n] + squares(g_other, i, j), -1, keepdims=True)
+        total_sq = jnp.sum(rb[n], -1, keepdims=True)
         rb[n] = jnp.broadcast_to(lax.rsqrt(total_sq * (1.0 / 4096) + 1e-05), (32, 128))
 
     loads[3].wait()
@@ -308,16 +363,15 @@
             gain = gain_ref[:, pl.ds(at, 128)]
             for n in range(8):
                 i, j = held(c, parity, n)
-                normed[n * 32 : (n + 1) * 32, pl.ds(at, 128)] = (ref[i, j, o].astype(F32) * rb[n] * gain).astype(BF16)
-
-    for half in range(2):
-        acc[half] = nt_dot(lm_buf[half, :, :512], normed[:, :512])
-
-    @pl.loop(1, 8)
-    def _(t):
-        lanes = pl.ds(pl.multiple_of(t * 512, 512), 512)
-        for half in range(2):
-            acc[half] += nt_dot(lm_buf[half, :, lanes], normed[:, lanes])
+                tile = (ref[i, j, o].astype(F32) * rb[n] * gain).astype(BF16)
+                normed[o, n * 32 : (n + 1) * 32, pl.ds(pl.multiple_of(parity * 128, 128), 128)] = tile
+        if o % 2:
+            for part in range(2):
+                grown = 0.0 if o == 1 else acc[part]
+                for k in (o - 1, o):
+                    lanes = pl.ds(pl.multiple_of(at_z(NEAR[k]) * 256, 256), 256)
+                    grown = grown + nt_dot(lm_buf[part, :, lanes], normed[k])
+                acc[part] = grown
 
     logits = [acc[0], acc[1]]
     peak = jnp.maximum(jnp.max(logits[0], 0, keepdims=True), jnp.max(logits[1], 0, keepdims=True))
@@ -457,7 +511,7 @@
             pltpu.VMEM((4, 4, 16, 32, 128), BF16),
             pltpu.VMEM((4, 4, 16, 32, 128), BF16),
             pltpu.VMEM((8, 32, 128), F32),
-            pltpu.VMEM((256, 4096), BF16),
+            pltpu.VMEM((16, 256, 256), BF16),
             pltpu.VMEM((2, 256, 256), F32),
             pltpu.VMEM((2, 2, 128), F32),
             pltpu.VMEM((16, 2, 128), F32),
@@ -465,13 +519,13 @@
             pltpu.VMEM((16, 2, 128), F32),
             dma((4,)), dma((8,)),
             dma((2,)), dma((2,)),
-            dma((14,)), dma((16,)),
-            dma((8,)), dma((8,)),
+            dma((28,)), dma((28,)),
+            dma((12,)), dma((12,)),
             dma((8,)), dma((8,)),
             dma((16,)), dma((16,)),
-            dma((12,)), dma((12,)),
-            dma((48,)), dma((48,)),
-            dma((8,)), dma((8,)),
+            dma((16,)), dma((16,)),
+            dma((64,)), dma((64,)),
+            dma((32,)), dma((32,)),
             dma((8,)), dma((16,)),
             dma((32,)), dma((16,)),
         ],

time: 89.5 us -> 89.1 us (level)
  no operation moved by 1% of the time
where the time goes in v3:
time: 89.1 us; the launch traced here: 88.9 us
  Pallas kernels  85.8 us (96%)
  local copies, waits for them, and re-layouts  2.46 us (3%)
    pallas_call x1, Pallas kernels, body(): pl.pallas_call(kernel, out_shape=jax.ShapeDtypeStruct((2, 128), F32), in_...  85.8 us

profile of v3, /device:TPU:1, one launch (start us, length us, event | category | flops | bytes accessed | tf_op | source)
XLA Modules:
  0.0 88.9 jit_solution(13120097112453668664)
XLA Ops:
  0.6 85.8 %shard_map.131 = f32[2,128]{1,0:T(2,128)} custom-call(bf16[1,4,1024]{2,1,0:T(4,128)(2,1)} %q_hbm.1, bf16[1,256,256]{2,1,0:T(8,128)(2,1)} %k_hbm.1, bf16[1,256,256]{2,1,0:T(8,128)(2,1)} %v_hbm.1, f32[32,128]{1,0:T(8,128)} %pos_hbm.1, bf16[4096,128]{1,0:T(8,128)(2,1)} %wk_hbm.1, bf16[4096,128]{1,0:T(8,128)(2,1)} %wv_hbm.1, bf16[1024,128]{1,0:T(8,128)(2,1)} %op_hbm.1, ...), custom_call_target="tpu_custom_call" | custom-call | tf_op jit(solution)/shard_map/pallas_call | solution.py:479
  86.4 1.3 %constant_dynamic-slice_fusion = f32[1,4]{1,0:T(1,128)} fusion(f32[2,128]{1,0:T(2,128)} %shard_map.131, s32[]{:T(128)S(6)} %select_n.3), kind=kLoop, calls=%fused_computation | loop fusion | bytes 36 | tf_op jit(solution)/shard_map/dynamic_slice | solution.py:540
  87.7 1.2 %slice.3 = f32[1,1]{1,0:T(1,128)} slice(f32[2,128]{1,0:T(2,128)} %shard_map.131), slice={[1:2], [0:1]} | slice | bytes 8 | tf_op jit(solution)/shard_map/slice | solution.py:541

commit v4 on v3

--- a/solution.py
+++ b/solution.py
@@ -25,6 +25,8 @@
 SLOT_OF = {off % NZ: k for k, off in enumerate(OFFSETS)}
 NEAR = (0, 1, -1, 2, -2, 3, -3, 4, -4, 5, -5, 6, -6, 7, -7, 8)
 CHUNK = 4
+MODE = 0
+ORDER = (1, 3, 2)
 CHUNKS = NZ // CHUNK
 LAST = CHUNKS - 1
 
@@ -273,33 +275,38 @@
     def slab2(d, e, part):
         return g_own.at[ring4(p2, (4 - d) % 4), ring4(p1, (4 - e) % 4), part]
 
+    def straight(send, part, base):
+        for d in ORDER:
+            if d == 2 and MODE == 2 and part < LAST:
+                send(half(part, 0), base + 2, 2)
+            else:
+                send(whole(part), base + SIDE[d], d)
+
     def send_first(s):
-        for d in (2, 1, 3) if s == LAST else (1, 3):
-            go(first(slab1(0, whole(s)), s * 4 + SIDE[d], d))
+        straight(lambda lines, i, d: go(first(slab1(0, lines), i, d)), s, s * 4)
 
     def send_second(s, e):
-        for d in (2, 1, 3) if s == LAST else (1, 3):
-            go(second(slab1(e, whole(s)), (s * 4 + e) * 4 + SIDE[d], d))
+        straight(lambda lines, i, d: go(second(slab1(e, lines), i, d)), s, (s * 4 + e) * 4)
 
     def on_first(s, e):
-        if e == 2 and s < LAST:
+        if e == 2 and MODE == 2 and s < LAST:
             for n in range(2):
                 first(slab1(2, half(s, n)), s * 4 + 2 + n, 1).wait_recv()
         else:
             first(slab1(e, whole(s)), s * 4 + SIDE[e], 1).wait_recv()
-            if s < LAST:
-                go(first(slab1(e, half(s, SIDE[e])), s * 4 + 2 + SIDE[e], e))
+            if e == 3 and MODE == 2 and s < LAST:
+                go(first(slab1(e, half(s, 1)), s * 4 + 3, e))
         send_second(s, e)
 
     def on_second(s, e, d):
         base = (s * 4 + e) * 4
-        if d == 2 and s < LAST:
+        if d == 2 and MODE == 2 and s < LAST:
             for n in range(2):
                 second(slab2(2, e, half(s, n)), base + 2 + n, 1).wait_recv()
         else:
             second(slab2(d, e, whole(s)), base + SIDE[d], 1).wait_recv()
-            if s < LAST:
-                go(second(slab2(d, e, half(s, SIDE[d])), base + 2 + SIDE[d], d))
+            if d == 3 and MODE == 2 and s < LAST:
+                go(second(slab2(d, e, half(s, 1)), base + 3, d))
 
     def on_origin(s):
         for o in range(max(1, s * CHUNK), (s + 1) * CHUNK):
@@ -328,23 +335,16 @@
             found = squares(g_own, s, c, c, n)
             rb[n] = found if s == 0 else rb[n] + found
 
-    events = []
     for s in range(CHUNKS):
-        start = 3.0 + 2.0 * s
-        twice = 3.5 if s == LAST else 5.6
-        events.append((start, s, 0, functools.partial(on_origin, s)))
-        latest = start
+        on_origin(s)
+    for s in range(CHUNKS):
+        for e in (1, 3, 2):
+            on_first(s, e)
+    for s in range(CHUNKS):
         for e in (0, 1, 3, 2):
-            ready = start + (0.0, 2.8, twice, 2.8)[e]
-            if e:
-                events.append((ready, s, 1, functools.partial(on_first, s, e)))
             for d in (1, 3, 2):
-                arrival = ready + (0.0, 2.8, twice, 2.8)[d]
-                latest = max(latest, arrival)
-                events.append((arrival, s, 2, functools.partial(on_second, s, e, d)))
-        events.append((latest, s, 3, functools.partial(on_complete, s)))
-    for event in sorted(events, key=lambda item: item[:3]):
-        event[3]()
+                on_second(s, e, d)
+        on_complete(s)
 
     for s in range(CHUNKS):
         for n in range(8):

time: 89.1 us -> 84.7 us (0.951)
  Pallas kernels: 85.8 us -> 81.4 us
    pallas_call x1, Pallas kernels: 85.8 us -> 81.4 us  [body(): pl.pallas_call(kernel, out_shape=jax.ShapeDtypeStruct((2, 128), F32), in_...]
where the time goes in v4:
time: 84.7 us; the launch traced here: 84.5 us
  Pallas kernels  81.4 us (96%)
  local copies, waits for them, and re-layouts  2.46 us (3%)
    pallas_call x1, Pallas kernels, body(): pl.pallas_call(kernel, out_shape=jax.ShapeDtypeStruct((2, 128), F32), in_...  81.4 us

profile of v4, /device:TPU:1, one launch (start us, length us, event | category | flops | bytes accessed | tf_op | source)
XLA Modules:
  0.0 84.5 jit_solution(6188874289863489333)
XLA Ops:
  0.6 81.4 %shard_map.131 = f32[2,128]{1,0:T(2,128)} custom-call(bf16[1,4,1024]{2,1,0:T(4,128)(2,1)} %q_hbm.1, bf16[1,256,256]{2,1,0:T(8,128)(2,1)} %k_hbm.1, bf16[1,256,256]{2,1,0:T(8,128)(2,1)} %v_hbm.1, f32[32,128]{1,0:T(8,128)} %pos_hbm.1, bf16[4096,128]{1,0:T(8,128)(2,1)} %wk_hbm.1, bf16[4096,128]{1,0:T(8,128)(2,1)} %wv_hbm.1, bf16[1024,128]{1,0:T(8,128)(2,1)} %op_hbm.1, ...), custom_call_target="tpu_custom_call" | custom-call | tf_op jit(solution)/shard_map/pallas_call | solution.py:479
  82.1 1.3 %constant_dynamic-slice_fusion = f32[1,4]{1,0:T(1,128)} fusion(f32[2,128]{1,0:T(2,128)} %shard_map.131, s32[]{:T(128)S(6)} %select_n.3), kind=kLoop, calls=%fused_computation | loop fusion | bytes 36 | tf_op jit(solution)/shard_map/dynamic_slice | solution.py:540
  83.3 1.2 %slice.3 = f32[1,1]{1,0:T(1,128)} slice(f32[2,128]{1,0:T(2,128)} %shard_map.131), slice={[1:2], [0:1]} | slice | bytes 8 | tf_op jit(solution)/shard_map/slice | solution.py:541

commit v5 on v4

--- a/solution.py
+++ b/solution.py
@@ -56,9 +56,6 @@
     peers = [(at_z(off), core, x, y) for off in range(1, NZ) for core in (0, 1)]
     peers += [(z, other, ring4(x, d), y) for d in range(4)]
     peers += [(z, c, ring4(x, d), ring4(y, e)) for d in range(4) for e in range(4) if d or e]
-    for peer in peers:
-        pl.semaphore_signal(barrier, inc=1, device_id=peer, device_id_type=MESH)
-
     loads = [
         pltpu.make_async_copy(wk_hbm, w_buf.at[0], local_sem.at[0]),
         pltpu.make_async_copy(wv_hbm, w_buf.at[1], local_sem.at[1]),
@@ -72,7 +69,11 @@
             (res_hbm, res_ref), (gain_hbm, gain_ref), (tgt_hbm, tgt_ref), (len_hbm, len_ref),
         ))
     ]
-    for load in small[:4] + loads + small[4:]:
+    for load in small[:4] + loads[:2]:
+        load.start()
+    for peer in peers:
+        pl.semaphore_signal(barrier, inc=1, device_id=peer, device_id_type=MESH)
+    for load in loads[2:] + small[4:]:
         load.start()
     for load in small[:4]:
         load.wait()
@@ -432,6 +433,9 @@
         f2(0, other, 1).start()
         zr[0] = fs[...]
 
+    for copy in sent:
+        copy.wait_send()
+
     for o in range(1, NZ):
         f2(o, c, 0).wait_recv()
 
@@ -450,8 +454,6 @@
     out_ref[0:1] = logprob
     out_ref[1:2] = jnp.broadcast_to(score, (1, 128))
 
-    for copy in sent:
-        copy.wait_send()
     for n in range(2):
         e = lax.rem(2 * c + n - y + 4, 4)
         for d in (2, 1, 3):

time: 84.7 us -> 84.4 us (level)
  no operation moved by 1% of the time
where the time goes in v5:
time: 84.4 us; the launch traced here: 84.3 us
  Pallas kernels  81.2 us (96%)
  local copies, waits for them, and re-layouts  2.46 us (3%)
    pallas_call x1, Pallas kernels, body(): pl.pallas_call(kernel, out_shape=jax.ShapeDtypeStruct((2, 128), F32), in_...  81.2 us

profile of v5, /device:TPU:1, one launch (start us, length us, event | category | flops | bytes accessed | tf_op | source)
XLA Modules:
  0.0 84.3 jit_solution(14143326144049867893)
XLA Ops:
  0.6 81.2 %shard_map.131 = f32[2,128]{1,0:T(2,128)} custom-call(bf16[1,4,1024]{2,1,0:T(4,128)(2,1)} %q_hbm.1, bf16[1,256,256]{2,1,0:T(8,128)(2,1)} %k_hbm.1, bf16[1,256,256]{2,1,0:T(8,128)(2,1)} %v_hbm.1, f32[32,128]{1,0:T(8,128)} %pos_hbm.1, bf16[4096,128]{1,0:T(8,128)(2,1)} %wk_hbm.1, bf16[4096,128]{1,0:T(8,128)(2,1)} %wv_hbm.1, bf16[1024,128]{1,0:T(8,128)(2,1)} %op_hbm.1, ...), custom_call_target="tpu_custom_call" | custom-call | tf_op jit(solution)/shard_map/pallas_call | solution.py:481
  81.8 1.3 %constant_dynamic-slice_fusion = f32[1,4]{1,0:T(1,128)} fusion(f32[2,128]{1,0:T(2,128)} %shard_map.131, s32[]{:T(128)S(6)} %select_n.3), kind=kLoop, calls=%fused_computation | loop fusion | bytes 36 | tf_op jit(solution)/shard_map/dynamic_slice | solution.py:542
  83.1 1.2 %slice.3 = f32[1,1]{1,0:T(1,128)} slice(f32[2,128]{1,0:T(2,128)} %shard_map.131), slice={[1:2], [0:1]} | slice | bytes 8 | tf_op jit(solution)/shard_map/slice | solution.py:543
